TPU v7x, 32 devices: a whole 2x2x4 slice. The times are simulated.
32 devices in a mesh: batch: 16 (over z, x, core), seq: 2 (over y).
Axes of the slice: x: 2, y: 2, z: 4, core: 2. Of those that a mesh axis runs over, the one named last changes fastest.
Arguments:
- tokens: bfloat16 [16, 1024, 2560], P('batch', 'seq'), may hold values from -6 to 6
- attn_in: bfloat16 [16, 1024, 2560], P('batch', 'seq'), may hold values from -6 to 6
- lengths: int32 [16], P('batch'), may hold values from 256 to 1024
- norm_gain: float32 [2560], replicated, may hold values from 0.5 to 1.5
- attn_gain: float32 [2560], replicated, may hold values from 0.5 to 1.5
- w_x: bfloat16 [2560, 2560], P(('batch', 'seq')), may hold values from -0.125 to 0.125
- conv_w: float32 [4, 2560], replicated, may hold values from -3 to 3
- w_a: bfloat16 [10, 256, 256], replicated, may hold values from -0.375 to 0.375
- w_i: bfloat16 [10, 256, 256], replicated, may hold values from -0.375 to 0.375
- lru_decay: float32 [2560], replicated, may hold values from 4 to 20
- w_kv: bfloat16 [2560, 512], replicated, may hold values from -0.125 to 0.125
Outputs:
- lru_state: float32 [16, 2560], P('batch', 'seq')
- conv_state: bfloat16 [16, 3, 2560], P('batch', None, 'seq')
- kv_cache: bfloat16 [16, 2048, 512], P('batch', None, 'seq')
Inputs may be any that keep to these rules, and one draw needn't show every extreme that they name: `lengths`: positions from a prompt's length on are padding.
All inputs are finite; a program needn't handle non-finite values.
Results may differ from a plain program's by a relative error of at most 0.0051.
Values may be sent and summed in bfloat16 or wider, within the bound.
A program may use at most 128 MiB of HBM per device.

v0:
```python
import functools

import jax
import jax.numpy as jnp
from jax import lax
from jax.experimental import pallas as pl
from jax.experimental.pallas import tpu as pltpu
from jax.sharding import PartitionSpec as P

H = 10
HD = 256
W = 2048
LANES_OF_TIME = 8
TAPS = 4
HALO = 16
STEP_ROWS = 32


def passed_along(block, axis, distance):
    devices = range(lax.axis_size(axis))
    route = [(i - distance, i) for i in devices if i - distance in devices]
    return lax.ppermute(block, axis, route)


def rms_norm(values, gain_vec):
    widened = values.astype(jnp.float32)
    inverse = lax.rsqrt(jnp.mean(widened * widened, axis=-1, keepdims=True) + 1e-06)
    return (widened * inverse * gain_vec).astype(jnp.bfloat16)


def rotate_keys(key_rows, positions):
    quarter = key_rows.shape[-1] // 4
    spacing = jnp.exp(-jnp.log(10000.0) * jnp.arange(quarter, dtype=jnp.float32) / quarter)
    angles = positions.astype(jnp.float32)[:, None] * spacing[None, :]
    cosine_rows = jnp.cos(angles)
    sine_rows = jnp.sin(angles)
    first_part = key_rows[:, :quarter]
    second_part = key_rows[:, quarter : 2 * quarter]
    return jnp.concatenate(
        [
            first_part * cosine_rows - second_part * sine_rows,
            second_part * cosine_rows + first_part * sine_rows,
            key_rows[:, 2 * quarter :],
        ],
        axis=1,
    )


def ordered_rows(tokens_ref, halo_ref, gain_ref, normed_ref):
    local_len = tokens_ref.shape[0]
    steps = local_len // LANES_OF_TIME
    row = lax.broadcasted_iota(jnp.int32, (normed_ref.shape[0], local_len + HALO), 0)
    col = lax.broadcasted_iota(jnp.int32, (normed_ref.shape[0], local_len + HALO), 1)
    at = lax.rem(row, LANES_OF_TIME) * steps + lax.div(row, LANES_OF_TIME) - (TAPS - 1)
    pick = (jnp.where(at < 0, at + local_len + HALO, at) == col).astype(jnp.bfloat16)
    rows = jnp.concatenate(
        [rms_norm(tokens_ref[...], gain_ref[...]), rms_norm(halo_ref[...], gain_ref[...])], axis=0
    )
    normed_ref[...] = jnp.dot(pick, rows, preferred_element_type=jnp.float32).astype(jnp.bfloat16)


def one_head(
    normed_ref, w_block, conv_w, w_a, w_i, rate, length, start, out_ref, xp_ref, xc_ref, ga_ref, gi_ref
):
    rows_ext = normed_ref.shape[0]
    local_len = xc_ref.shape[0]
    steps = local_len // LANES_OF_TIME
    projected = jnp.dot(normed_ref[...], w_block, preferred_element_type=jnp.float32).astype(
        jnp.bfloat16
    )
    xp_ref[...] = projected.astype(jnp.float32)
    row = lax.broadcasted_iota(jnp.int32, (HALO, rows_ext), 1)
    wanted = length - (TAPS - 1) + lax.broadcasted_iota(jnp.int32, (HALO, rows_ext), 0) - 2
    step = lax.div(row, LANES_OF_TIME) - (TAPS - 1)
    at = start + lax.rem(row, LANES_OF_TIME) * steps + step
    real = (step >= 0) & (step < steps) & (wanted < length) & (wanted >= length - (TAPS - 1))
    picker = (real & (at == wanted)).astype(jnp.bfloat16)
    picked = jnp.dot(picker, projected, preferred_element_type=jnp.float32)
    conv_sum = conv_w[0:1] * xp_ref[0:local_len]
    for offset in range(1, TAPS):
        shift = offset * LANES_OF_TIME
        conv_sum = conv_sum + conv_w[offset : offset + 1] * xp_ref[shift : shift + local_len]
    x_conv = conv_sum.astype(jnp.bfloat16)
    xc_ref[...] = x_conv.astype(jnp.float32)
    ga_ref[...] = jnp.dot(x_conv, w_a, preferred_element_type=jnp.float32)
    gi_ref[...] = jnp.dot(x_conv, w_i, preferred_element_type=jnp.float32)
    inner = lax.broadcasted_iota(jnp.int32, (STEP_ROWS, HD), 0)
    first_at = start + lax.rem(inner, LANES_OF_TIME) * steps + lax.div(inner, LANES_OF_TIME)

    def block(i, carry):
        state, rate_sum = carry
        rows = pl.ds(pl.multiple_of(i * STEP_ROWS, STEP_ROWS), STEP_ROWS)
        valid = first_at + i * (STEP_ROWS // LANES_OF_TIME) < length
        log_rate = rate * jax.nn.sigmoid(ga_ref[rows])
        fall = -2.0 * log_rate
        lost = 1.0 - fall * (1.0 / 6.0)
        for order in (5.0, 4.0, 3.0, 2.0):
            lost = 1.0 - fall * (1.0 / order) * lost
        lost = fall * lost
        root = lost * lax.rsqrt(jnp.maximum(lost, 1e-37))
        push = jnp.where(valid, root * jax.nn.sigmoid(gi_ref[rows]) * xc_ref[rows], 0.0)
        held = jnp.where(valid, log_rate, 0.0)
        keep = jnp.exp(held)
        for k in range(STEP_ROWS // LANES_OF_TIME):
            tile = slice(k * LANES_OF_TIME, (k + 1) * LANES_OF_TIME)
            state = keep[tile] * state + push[tile]
            rate_sum = rate_sum + held[tile]
        return state, rate_sum

    zeros = jnp.zeros((LANES_OF_TIME, HD), jnp.float32)
    state, rate_sum = lax.fori_loop(0, local_len // STEP_ROWS, block, (zeros, zeros))
    keep_all = jnp.exp(rate_sum)
    total = state[0:1]
    for s in range(1, LANES_OF_TIME):
        total = keep_all[s : s + 1] * total + state[s : s + 1]
    keep_total = jnp.exp(jnp.sum(rate_sum, axis=0, keepdims=True))
    place = lax.broadcasted_iota(jnp.int32, (LANES_OF_TIME, HD), 0)
    out_ref[...] = jnp.where(
        place == 0, keep_total, jnp.where(place == 1, total, picked[0:LANES_OF_TIME])
    )


def recurrent_kernel(
    length_ref,
    tokens_ref,
    halo_ref,
    gain_ref,
    w_ref,
    conv_ref,
    wa_ref,
    wi_ref,
    rate_ref,
    out_ref,
    normed_ref,
    *work
):
    @pl.when(pl.program_id(0) == 0)
    def _():
        ordered_rows(tokens_ref, halo_ref, gain_ref, normed_ref)

    start = lax.axis_index("seq") * tokens_ref.shape[0]
    one_head(
        normed_ref,
        w_ref[...],
        conv_ref[...],
        wa_ref[0],
        wi_ref[0],
        rate_ref[...],
        length_ref[0],
        start,
        out_ref,
        *work
    )


def recurrent(tokens, halo, lengths, norm_gain, w_full, conv_w, w_a, w_i, rate):
    local_len, width = tokens.shape
    rows_ext = -(-(local_len + (TAPS - 1) * LANES_OF_TIME) // HALO) * HALO
    whole = lambda *shape: pl.BlockSpec(shape, lambda h: (0,) * len(shape))
    return pl.pallas_call(
        recurrent_kernel,
        grid=(width // HD,),
        in_specs=[
            pl.BlockSpec(memory_space=pltpu.SMEM),
            whole(local_len, width),
            whole(HALO, width),
            whole(1, width),
            pl.BlockSpec((width, HD), lambda h: (0, h)),
            pl.BlockSpec((TAPS, HD), lambda h: (0, h)),
            pl.BlockSpec((1, HD, HD), lambda h: (h, 0, 0)),
            pl.BlockSpec((1, HD, HD), lambda h: (h, 0, 0)),
            pl.BlockSpec((1, HD), lambda h: (0, h)),
        ],
        out_specs=pl.BlockSpec((LANES_OF_TIME, HD), lambda h: (0, h)),
        out_shape=jax.ShapeDtypeStruct((LANES_OF_TIME, width), jnp.float32),
        scratch_shapes=[
            pltpu.VMEM((rows_ext, width), jnp.bfloat16),
            pltpu.VMEM((rows_ext, HD), jnp.float32),
            pltpu.VMEM((local_len, HD), jnp.float32),
            pltpu.VMEM((local_len, HD), jnp.float32),
            pltpu.VMEM((local_len, HD), jnp.float32),
        ],
        compiler_params=pltpu.CompilerParams(vmem_limit_bytes=48 * 1024 * 1024),
    )(lengths, tokens, halo, norm_gain[None], w_full, conv_w, w_a, w_i, rate[None])


def on_device(
    tokens, attn_in, lengths, norm_gain, attn_gain, w_x, conv_w, w_a, w_i, lru_decay, w_kv
):
    local_len = tokens.shape[1]
    feature_dim = tokens.shape[2]
    seq_parts = lax.axis_size("seq")
    seq_place = lax.axis_index("seq")
    length = lengths[0]
    halo = passed_along(tokens[0, local_len - HALO :], "seq", 1)
    w_full = lax.all_gather(w_x, ("batch", "seq"), axis=0, tiled=True)
    positions = seq_place * local_len + jnp.arange(local_len, dtype=jnp.int32)
    attn_normed = rms_norm(attn_in[0], attn_gain)
    kv_full = jnp.dot(attn_normed, w_kv, preferred_element_type=jnp.float32)
    kv_rows = jnp.concatenate(
        [rotate_keys(kv_full[:, :HD], positions), kv_full[:, HD:]], axis=1
    ).astype(jnp.bfloat16)
    in_window = ((positions >= length - W) & (positions < length))[:, None]
    masked = jnp.where(in_window, kv_rows, jnp.zeros_like(kv_rows))
    by_column = lax.all_to_all(masked, "seq", split_axis=1, concat_axis=0, tiled=True)
    laps = -(-seq_parts * local_len // W)
    by_column = jnp.pad(by_column, ((0, laps * W - seq_parts * local_len), (0, 0)))
    kv_cache = by_column[:W]
    for lap in range(1, laps):
        kv_cache = kv_cache + by_column[lap * W : (lap + 1) * W]
    rate = -8.0 * jax.nn.softplus(-lru_decay)
    summary = recurrent(tokens[0], halo, lengths, norm_gain, w_full, conv_w, w_a, w_i, rate)
    owned = lax.all_to_all(
        summary.reshape(1, LANES_OF_TIME, feature_dim), "seq", split_axis=2, concat_axis=0, tiled=True
    )
    state = owned[0, 1]
    for part in range(1, seq_parts):
        state = owned[part, 0] * state + owned[part, 1]
    conv_state = jnp.sum(owned[:, 2:5], axis=0).astype(jnp.bfloat16)
    return (state[None], conv_state[None], kv_cache[None])


def solution(mesh):
    in_specs = (
        P("batch", "seq", None),
        P("batch", "seq", None),
        P("batch"),
        P(),
        P(),
        P(("batch", "seq"), None),
        P(),
        P(),
        P(),
        P(),
        P(),
    )
    out_specs = (P("batch", "seq"), P("batch", None, "seq"), P("batch", None, "seq"))
    return jax.shard_map(
        on_device, mesh=mesh, in_specs=in_specs, out_specs=out_specs, check_vma=False
    )
```

profile of v0, /device:TPU:0, one launch (start us, length us, event | category | flops | bytes accessed | tf_op | source)
XLA Modules:
  0.0 186.6 jit_solution(208620327275275955)
XLA Ops:
  7.2 0.0 copy-start
  7.2 0.0 all-gather.2.cloned.1.call-start
  7.2 0.7 all-gather.2.cloned.1.call-update
  8.7 2.4 %fusion = f32[512]{0:T(512)S(1)} fusion(bf16[1,512,2560]{2,1,0:T(8,128)(2,1)} %param.12), kind=kLoop, calls=%fused_computation.2 | loop fusion | flops 3931648 | bytes 2623488 | tf_op jit(solution)/shard_map/reduce_sum | solution.py:27
  11.1 1.7 fusion.3
  12.8 0.0 copy-start.7
  12.8 1.0 copy-done.7
  13.9 1.5 fusion.13
  15.5 0.8 broadcast_select_fusion
  16.3 4.3 %all-to-all-start.1 = ((bf16[512,2,256]{0,2,1:T(8,128)(2,1)}), bf16[512,2,256]{0,2,1:T(8,128)(2,1)S(1)}, u32[]{:S(2)}, u32[]{:S(2)}) async-start(bf16[512,2,256]{0,2,1:T(8,128)(2,1)} %broadcast_select_fusion), calls=%async_computation.1 | async-start | bytes 1048576 | tf_op jit(solution)/shard_map/all_to_all | solution.py:205
  20.6 0.9 slice_bitcast_fusion
  21.5 4.1 %collective-permute-start = (bf16[16,2560]{1,0:T(8,128)(2,1)S(1)}, bf16[16,2560]{1,0:T(8,128)(2,1)S(1)}, u32[]{:S(2)}, u32[]{:S(2)}) collective-permute-start(bf16[16,2560]{1,0:T(8,128)(2,1)S(1)} %slice_bitcast_fusion), channel_id=1, source_target_pairs={{0,1},{2,3},{4,5},{6,7},{8,9},{10,11},{12,13},{14,15},{16,17},{18,... | collective-permute-start | bytes 245768 | tf_op jit(solution)/shard_map/ppermute | solution.py:22
  25.7 6.5 %all-to-all-done.1 = bf16[512,2,256]{0,2,1:T(8,128)(2,1)S(1)} async-done(((bf16[512,2,256]{0,2,1:T(8,128)(2,1)}), bf16[512,2,256]{0,2,1:T(8,128)(2,1)S(1)}, u32[]{:S(2)}, u32[]{:S(2)}) %all-to-all-start.1) | async-done | bytes 524320 | tf_op jit(solution)/shard_map/all_to_all | solution.py:205
  32.2 0.8 copy-done.6
  33.0 1.2 copy.19
  34.3 79.3 %all-gather.2.cloned.1.call-done.w_ref = bf16[2560,2560]{1,0:T(8,128)(2,1)} async-done(((bf16[80,2560]{1,0:T(8,128)(2,1)}), bf16[2560,2560]{1,0:T(8,128)(2,1)}) %all-gather.2.cloned.1.call-update) | async-done | bytes 13107216 | tf_op jit(solution)/shard_map/all_gather | solution.py:196
  113.6 1.7 copy-done.1
  115.3 1.3 copy-done.2
  116.6 1.3 copy-done.3
  118.0 28.1 %shard_map.130 = f32[8,2560]{1,0:T(8,128)S(1)} custom-call(s32[1]{0:T(128)} %copy.20.length_ref, bf16[512,2560]{1,0:T(8,128)(2,1)S(1)} %bitcast.31, bf16[16,2560]{1,0:T(8,128)(2,1)S(1)} %collective-permute-done.halo_ref, f32[1,2560]{1,0:T(1,128)S(1)} %broadcast_in_dim.16.gain_ref, bf16[2560,2560]{1,0:T(8,128)(2,1)} %all-gather.2.cloned.1.call-done.w_ref, ...), custom_call_target="tpu_custom_call" | custom-call | tf_op jit(solution)/shard_map/pallas_call | solution.py:160
  146.1 2.0 %copy.17 = f32[1,8,2560]{1,0,2:T(1,128)} copy(f32[1,8,2560]{2,1,0:T(8,128)S(1)} %bitcast.32) | data formatting | bytes 163840 | tf_op jit(solution)/shard_map/reshape | solution.py:214
  148.1 0.5 broadcast.41
  148.6 14.1 %reduce = f32[2560,8]{1,0:T(8,128)} reduce(f32[2560,1,8]{2,1,0:T(1,128)} %bitcast.33, f32[]{:T(128)} %broadcast.41), dimensions={1}, to_apply=%bitcast.26.reduce_sub_computation | reduce | bytes 163844
  162.7 2.6 %reshape.84 = f32[2,1,10240]{2,1,0:T(1,128)} reshape(f32[2560,8]{1,0:T(8,128)} %reduce) | data formatting | bytes 163840
  165.3 3.3 %all-to-all-start = ((f32[2,1,10240]{2,1,0:T(1,128)}), f32[2,1,10240]{2,1,0:T(1,128)S(1)}, u32[]{:S(2)}, u32[]{:S(2)}) async-start(f32[2,1,10240]{2,1,0:T(1,128)} %reshape.84), calls=%async_computation | async-start | bytes 163840 | tf_op jit(solution)/shard_map/all_to_all | solution.py:213
  168.6 1.0 pad_bitcast_fusion
  169.6 3.2 %all-to-all-done = f32[2,1,10240]{2,1,0:T(1,128)S(1)} async-done(((f32[2,1,10240]{2,1,0:T(1,128)}), f32[2,1,10240]{2,1,0:T(1,128)S(1)}, u32[]{:S(2)}, u32[]{:S(2)}) %all-to-all-start) | async-done | bytes 81952 | tf_op jit(solution)/shard_map/all_to_all | solution.py:213
  172.8 0.9 reduce.1
  173.7 3.2 %reshape.85 = f32[2560,1,8]{2,1,0:T(1,128)} reshape(f32[2,10240]{1,0:T(2,128)S(1)} %reduce.1) | data formatting | bytes 163840
  176.8 1.7 copy.18
  178.5 0.6 fusion.17
  179.1 0.6 slice_reduce_fusion
  (25 shorter events, 0.2 us)
Async XLA Ops:
  7.2 3.9 %copy-start = (bf16[2560,512]{1,0:T(8,128)(2,1)S(1)}, bf16[2560,512]{1,0:T(8,128)(2,1)}, u32[]{:S(2)}) copy-start(bf16[2560,512]{1,0:T(8,128)(2,1)} %param.21) | copy-start | bytes 7864324
  7.2 3.9 %copy-start.10 = (f32[2560]{0:T(1024)S(1)}, f32[2560]{0:T(1024)}, u32[]{:S(2)}) copy-start(f32[2560]{0:T(1024)} %param.15) | copy-start | bytes 30724
  7.2 106.4 %all-gather.2.cloned.1.call-start = ((), (), s32[]{:S(2)}) async-start(), calls=%async_computation.2 | async-start | bytes 13516800 | tf_op jit(solution)/shard_map/all_gather | solution.py:196
  7.9 3.2 %copy-start.5 = (bf16[1,512,2560]{2,1,0:T(8,128)(2,1)S(1)}, bf16[1,512,2560]{2,1,0:T(8,128)(2,1)}, u32[]{:S(2)}) copy-start(bf16[1,512,2560]{2,1,0:T(8,128)(2,1)} %param.12) | copy-start | bytes 7864324
  12.8 1.0 copy-start.7
  13.8 11.8 %copy-start.8 = (f32[2560]{0:T(1024)S(1)}, f32[2560]{0:T(1024)}, u32[]{:S(2)}) copy-start(f32[2560]{0:T(1024)} %param.20) | copy-start | bytes 30724
  13.8 11.9 %copy-start.9 = (f32[2560]{0:T(1024)S(1)}, f32[2560]{0:T(1024)}, u32[]{:S(2)}) copy-start(f32[2560]{0:T(1024)} %param.14) | copy-start | bytes 30724
  13.8 99.8 %copy-start.4 = (f32[4,2560]{1,0:T(4,128)S(1)}, f32[4,2560]{1,0:T(4,128)}, u32[]{:S(2)}) copy-start(f32[4,2560]{1,0:T(4,128)} %conv_ref.1) | copy-start | bytes 122884
  16.3 15.9 %all-to-all-start.1 = ((bf16[512,2,256]{0,2,1:T(8,128)(2,1)}), bf16[512,2,256]{0,2,1:T(8,128)(2,1)S(1)}, u32[]{:S(2)}, u32[]{:S(2)}) async-start(bf16[512,2,256]{0,2,1:T(8,128)(2,1)} %broadcast_select_fusion), calls=%async_computation.1 | async-start | bytes 1048576 | tf_op jit(solution)/shard_map/all_to_all | solution.py:205
  21.5 12.8 %collective-permute-start = (bf16[16,2560]{1,0:T(8,128)(2,1)S(1)}, bf16[16,2560]{1,0:T(8,128)(2,1)S(1)}, u32[]{:S(2)}, u32[]{:S(2)}) collective-permute-start(bf16[16,2560]{1,0:T(8,128)(2,1)S(1)} %slice_bitcast_fusion), channel_id=1, source_target_pairs={{0,1},{2,3},{4,5},{6,7},{8,9},{10,11},{12,13},{14,15},{16,17},{18,... | collective-permute-start | bytes 245768 | tf_op jit(solution)/shard_map/ppermute | solution.py:22
  32.2 0.8 copy-start.6
  113.6 1.7 copy-start.1
  115.3 1.3 copy-start.2
  116.6 1.3 copy-start.3
  165.3 7.5 %all-to-all-start = ((f32[2,1,10240]{2,1,0:T(1,128)}), f32[2,1,10240]{2,1,0:T(1,128)S(1)}, u32[]{:S(2)}, u32[]{:S(2)}) async-start(f32[2,1,10240]{2,1,0:T(1,128)} %reshape.84), calls=%async_computation | async-start | bytes 163840 | tf_op jit(solution)/shard_map/all_to_all | solution.py:213
Sparse Core Ops, SparseCore 0:
  10.8 102.6 all-gather.1
where the time goes:
time: 187 us
  waiting for transfers between devices  89.7 us (48%)
  Pallas kernels  28.1 us (15%)
  other arithmetic  21 us (11%)
  local copies, waits for them, and re-layouts  19.3 us (10%)
  between operations  15 us (8%)
  starting transfers between devices  11.7 us (6%)
    all_gather x1, waiting for transfers between devices, on_device(): w_full = lax.all_gather(w_x, ('batch', 'seq'), axis=0, tiled=True)  79.3 us
    pallas_call x1, Pallas kernels, recurrent(): pl.pallas_call(recurrent_kernel, grid=(width // HD,), in_specs=[pl.BlockS...  28.1 us
    unnamed x1, other arithmetic  14.1 us
    unnamed x25, local copies, waits for them, and re-layouts  12.4 us
    all_to_all x1, waiting for transfers between devices, on_device(): lax.all_to_all(masked, 'seq', split_axis=1, concat_axis=0, tiled=True)  6.53 us
    all_to_all x1, starting transfers between devices, on_device(): lax.all_to_all(masked, 'seq', split_axis=1, concat_axis=0, tiled=True)  4.26 us
    ppermute x1, starting transfers between devices, passed_along(): return lax.ppermute(block, axis, route)  4.12 us
  transfers between devices with their start and end apart: 4, of which 3 were waited for; matrix products, arithmetic and copies ran while one was open for 5% of the time, Pallas kernels for 0%

commit v1 on v0

--- a/solution.py
+++ b/solution.py
@@ -153,26 +153,27 @@
     )
 
 
-def recurrent(tokens, halo, lengths, norm_gain, w_full, conv_w, w_a, w_i, rate):
+def recurrent(first, tokens, halo, lengths, norm_gain, w_part, conv_w, w_a, w_i, rate):
     local_len, width = tokens.shape
+    part_width = w_part.shape[1]
     rows_ext = -(-(local_len + (TAPS - 1) * LANES_OF_TIME) // HALO) * HALO
     whole = lambda *shape: pl.BlockSpec(shape, lambda h: (0,) * len(shape))
     return pl.pallas_call(
         recurrent_kernel,
-        grid=(width // HD,),
+        grid=(part_width // HD,),
         in_specs=[
             pl.BlockSpec(memory_space=pltpu.SMEM),
             whole(local_len, width),
             whole(HALO, width),
             whole(1, width),
             pl.BlockSpec((width, HD), lambda h: (0, h)),
-            pl.BlockSpec((TAPS, HD), lambda h: (0, h)),
-            pl.BlockSpec((1, HD, HD), lambda h: (h, 0, 0)),
-            pl.BlockSpec((1, HD, HD), lambda h: (h, 0, 0)),
-            pl.BlockSpec((1, HD), lambda h: (0, h)),
+            pl.BlockSpec((TAPS, HD), lambda h: (0, h + first)),
+            pl.BlockSpec((1, HD, HD), lambda h: (h + first, 0, 0)),
+            pl.BlockSpec((1, HD, HD), lambda h: (h + first, 0, 0)),
+            pl.BlockSpec((1, HD), lambda h: (0, h + first)),
         ],
         out_specs=pl.BlockSpec((LANES_OF_TIME, HD), lambda h: (0, h)),
-        out_shape=jax.ShapeDtypeStruct((LANES_OF_TIME, width), jnp.float32),
+        out_shape=jax.ShapeDtypeStruct((LANES_OF_TIME, part_width), jnp.float32),
         scratch_shapes=[
             pltpu.VMEM((rows_ext, width), jnp.bfloat16),
             pltpu.VMEM((rows_ext, HD), jnp.float32),
@@ -180,8 +181,13 @@
             pltpu.VMEM((local_len, HD), jnp.float32),
             pltpu.VMEM((local_len, HD), jnp.float32),
         ],
-        compiler_params=pltpu.CompilerParams(vmem_limit_bytes=48 * 1024 * 1024),
-    )(lengths, tokens, halo, norm_gain[None], w_full, conv_w, w_a, w_i, rate[None])
+        compiler_params=pltpu.CompilerParams(vmem_limit_bytes=60 * 1024 * 1024),
+        cost_estimate=pl.CostEstimate(
+            flops=2 * local_len * part_width * (width + 2 * HD),
+            bytes_accessed=2 * width * (local_len + part_width),
+            transcendentals=6 * local_len * part_width,
+        ),
+    )(lengths, tokens, halo, norm_gain[None], w_part, conv_w, w_a, w_i, rate[None])
 
 
 def on_device(
@@ -193,7 +199,8 @@
     seq_place = lax.axis_index("seq")
     length = lengths[0]
     halo = passed_along(tokens[0, local_len - HALO :], "seq", 1)
-    w_full = lax.all_gather(w_x, ("batch", "seq"), axis=0, tiled=True)
+    heads = feature_dim // HD
+    early = (4 * heads) // 5
     positions = seq_place * local_len + jnp.arange(local_len, dtype=jnp.int32)
     attn_normed = rms_norm(attn_in[0], attn_gain)
     kv_full = jnp.dot(attn_normed, w_kv, preferred_element_type=jnp.float32)
@@ -208,16 +215,29 @@
     kv_cache = by_column[:W]
     for lap in range(1, laps):
         kv_cache = kv_cache + by_column[lap * W : (lap + 1) * W]
+    w_early = lax.all_gather(w_x[:, : early * HD], ("batch", "seq"), axis=0, tiled=True)
+    w_early, w_local, kv_cache, halo = lax.optimization_barrier((w_early, w_x, kv_cache, halo))
+    w_late = lax.all_gather(w_local[:, early * HD :], ("batch", "seq"), axis=0, tiled=True)
+    w_parts = ((0, w_early), (early, w_late))
     rate = -8.0 * jax.nn.softplus(-lru_decay)
-    summary = recurrent(tokens[0], halo, lengths, norm_gain, w_full, conv_w, w_a, w_i, rate)
-    owned = lax.all_to_all(
-        summary.reshape(1, LANES_OF_TIME, feature_dim), "seq", split_axis=2, concat_axis=0, tiled=True
-    )
-    state = owned[0, 1]
+    summary = jnp.concatenate(
+        [
+            recurrent(first, tokens[0], halo, lengths, norm_gain, w_part, conv_w, w_a, w_i, rate)
+            for first, w_part in w_parts
+        ],
+        axis=1,
+    )
+    owned_width = feature_dim // seq_parts
+    gathered = lax.all_gather(summary, "seq", axis=0, tiled=True)
+    owned = lax.dynamic_slice_in_dim(gathered, seq_place * owned_width, owned_width, 1)
+    state = owned[1:2]
+    picked = owned[2:5]
     for part in range(1, seq_parts):
-        state = owned[part, 0] * state + owned[part, 1]
-    conv_state = jnp.sum(owned[:, 2:5], axis=0).astype(jnp.bfloat16)
-    return (state[None], conv_state[None], kv_cache[None])
+        at = part * LANES_OF_TIME
+        state = owned[at : at + 1] * state + owned[at + 1 : at + 2]
+        picked = picked + owned[at + 2 : at + 5]
+    conv_state = picked.astype(jnp.bfloat16)
+    return (state, conv_state[None], kv_cache[None])
 
 
 def solution(mesh):

time: 187 us -> 186 us (level)
  other arithmetic: 21 us -> 7.04 us
  waiting for transfers between devices: 89.7 us -> 103 us
  local copies, waits for them, and re-layouts: 19.3 us -> 9.65 us
  Pallas kernels: 28.1 us -> 36.1 us
  blocking collectives: 0 us -> 5.22 us
  starting transfers between devices: 11.7 us -> 8.48 us
    all_gather x1 -> x2, waiting for transfers between devices: 79.3 us -> 96.8 us  [the longest x1 65.6 us: on_device(): lax.all_gather(w_x[:, :early * HD], ('batch', 'seq'), axis=0, tiled=True)]
    unnamed x1 -> x0, other arithmetic: 14.1 us -> none
    unnamed x25 -> x16, local copies, waits for them, and re-layouts: 12.4 us -> 1.02 us
    pallas_call x1 -> x2, Pallas kernels: 28.1 us -> 36.1 us  [recurrent(): pl.pallas_call(recurrent_kernel, grid=(part_width // HD,), in_specs=[pl.B...]
    all_gather x0 -> x1, blocking collectives: none -> 5.22 us  [on_device(): gathered = lax.all_gather(summary, 'seq', axis=0, tiled=True)]
    slice x0 -> x2, local copies, waits for them, and re-layouts: none -> 3.39 us  [the longest x1 1.87 us: on_device(): w_x[:, :early * HD]]
    all_to_all x1 -> x0, starting transfers between devices: 3.32 us -> none  [on_device(): lax.all_to_all(summary.reshape(1, LANES_OF_TIME, feature_dim), 'seq', spl...]
    all_to_all x1 -> x0, waiting for transfers between devices: 3.15 us -> none  [on_device(): lax.all_to_all(summary.reshape(1, LANES_OF_TIME, feature_dim), 'seq', spl...]
  transfers between devices with their start and end apart: 4 -> 4, of which waited for: 3 -> 3; matrix products, arithmetic and copies ran while one was open for 5% -> 6% of each run, Pallas kernels for 0% -> 14%
where the time goes in v1:
time: 186 us
  waiting for transfers between devices  103 us (55%)
  Pallas kernels  36.1 us (19%)
  between operations  14.8 us (8%)
  local copies, waits for them, and re-layouts  9.65 us (5%)
  starting transfers between devices  8.48 us (5%)
  other arithmetic  7.04 us (4%)
  blocking collectives  5.22 us (3%)
    all_gather x1, waiting for transfers between devices, on_device(): lax.all_gather(w_x[:, :early * HD], ('batch', 'seq'), axis=0, tiled=True)  65.6 us
    pallas_call x2, Pallas kernels, recurrent(): pl.pallas_call(recurrent_kernel, grid=(part_width // HD,), in_specs=[pl.B...  36.1 us
    all_gather x1, waiting for transfers between devices, on_device(): lax.all_gather(w_local[:, early * HD:], ('batch', 'seq'), axis=0, tiled=T...  31.2 us
    all_to_all x1, waiting for transfers between devices, on_device(): lax.all_to_all(masked, 'seq', split_axis=1, concat_axis=0, tiled=True)  5.99 us
    all_gather x1, blocking collectives, on_device(): gathered = lax.all_gather(summary, 'seq', axis=0, tiled=True)  5.22 us
    all_to_all x1, starting transfers between devices, on_device(): lax.all_to_all(masked, 'seq', split_axis=1, concat_axis=0, tiled=True)  4.26 us
    ppermute x1, starting transfers between devices, passed_along(): return lax.ppermute(block, axis, route)  4.18 us
  transfers between devices with their start and end apart: 4, of which 3 were waited for; matrix products, arithmetic and copies ran while one was open for 6% of the time, Pallas kernels for 14%

profile of v1, /device:TPU:0, one launch (start us, length us, event | category | flops | bytes accessed | tf_op | source)
XLA Modules:
  0.0 185.7 jit_solution(8690938932169258410)
XLA Ops:
  7.2 0.0 copy-start
  7.2 0.0 all-gather.3.cloned.1.call-start
  7.2 1.9 %slice.40 = bf16[80,2048]{1,0:T(8,128)(2,1)} slice(bf16[80,2560]{1,0:T(8,128)(2,1)} %param.16), slice={[0:80], [0:2048]} | slice | bytes 655360 | tf_op jit(solution)/shard_map/slice | solution.py:218
  9.1 0.0 all-gather.3.cloned.1.call-update
  9.1 0.0 copy-start.1
  9.1 2.5 %fusion = f32[512]{0:T(512)S(1)} fusion(bf16[1,512,2560]{2,1,0:T(8,128)(2,1)} %param.12), kind=kLoop, calls=%fused_computation.2 | loop fusion | flops 3931648 | bytes 2623488 | tf_op jit(solution)/shard_map/reduce_sum | solution.py:27
  11.7 0.0 copy-done.1
  11.7 1.7 fusion.3
  13.3 0.0 copy-start.2
  13.3 1.0 copy-done.2
  15.0 1.5 fusion.13
  16.6 0.0 copy-start.5
  16.6 0.0 copy-start.6
  16.7 0.8 broadcast_select_fusion
  17.5 4.3 %all-to-all-start = ((bf16[512,2,256]{0,2,1:T(8,128)(2,1)}), bf16[512,2,256]{0,2,1:T(8,128)(2,1)S(1)}, u32[]{:S(2)}, u32[]{:S(2)}) async-start(bf16[512,2,256]{0,2,1:T(8,128)(2,1)} %broadcast_select_fusion), calls=%async_computation | async-start | bytes 1048576 | tf_op jit(solution)/shard_map/all_to_all | solution.py:212
  21.8 0.9 slice_bitcast_fusion
  22.7 4.2 %collective-permute-start = (bf16[16,2560]{1,0:T(8,128)(2,1)S(1)}, bf16[16,2560]{1,0:T(8,128)(2,1)S(1)}, u32[]{:S(2)}, u32[]{:S(2)}) collective-permute-start(bf16[16,2560]{1,0:T(8,128)(2,1)S(1)} %slice_bitcast_fusion), channel_id=1, source_target_pairs={{0,1},{2,3},{4,5},{6,7},{8,9},{10,11},{12,13},{14,15},{16,17},{18,... | collective-permute-start | bytes 245768 | tf_op jit(solution)/shard_map/ppermute | solution.py:22
  26.8 6.0 %all-to-all-done = bf16[512,2,256]{0,2,1:T(8,128)(2,1)S(1)} async-done(((bf16[512,2,256]{0,2,1:T(8,128)(2,1)}), bf16[512,2,256]{0,2,1:T(8,128)(2,1)S(1)}, u32[]{:S(2)}, u32[]{:S(2)}) %all-to-all-start) | async-done | bytes 524320 | tf_op jit(solution)/shard_map/all_to_all | solution.py:212
  32.8 1.0 copy.14
  33.8 2.1 %pad.4 = bf16[2048,256]{1,0:T(8,128)(2,1)} pad(bf16[1024,256]{1,0:T(8,128)(2,1)} %bitcast.24, bf16[]{:T(256)} %constant.11.clone.1), padding=0_1024x0_0 | pad | bytes 1572866 | tf_op jit(solution)/shard_map/jit(_pad)/pad | solution.py:214
  35.9 65.6 %all-gather.3.cloned.1.call-done.w_ref = bf16[2560,2048]{1,0:T(8,128)(2,1)} async-done(((bf16[80,2048]{1,0:T(8,128)(2,1)}), bf16[2560,2048]{1,0:T(8,128)(2,1)}) %all-gather.3.cloned.1.call-update) | async-done | bytes 10485776 | tf_op jit(solution)/shard_map/all_gather | solution.py:218
  101.5 1.5 slice.45
  103.0 0.0 all-gather.5.cloned.1.call-update
  103.1 0.6 broadcast_in_dim.33.rate_ref
  103.7 0.6 broadcast_in_dim.32.gain_ref
  104.3 25.3 %shard_map.130 = f32[8,2048]{1,0:T(8,128)} custom-call(s32[1]{0:T(128)} %copy.15.length_ref, bf16[512,2560]{1,0:T(8,128)(2,1)} %bitcast.20, bf16[16,2560]{1,0:T(8,128)(2,1)} %copy-done.3, f32[1,2560]{1,0:T(1,128)} %broadcast_in_dim.32.gain_ref, bf16[2560,2048]{1,0:T(8,128)(2,1)} %all-gather.3.cloned.1.call-done.w_ref, f32[4,2560]{1,0:T(4,128)} %conv_ref.3, ...), custom_call_target="tpu_custom_call" | custom-call | flops 6442450944 | bytes 13107200 | tf_op jit(solution)/shard_map/pallas_call | solution.py:161
  129.6 31.2 %all-gather.5.cloned.1.call-done.w_ref = bf16[2560,512]{1,0:T(8,128)(2,1)} async-done(((bf16[80,512]{1,0:T(8,128)(2,1)}), bf16[2560,512]{1,0:T(8,128)(2,1)}) %all-gather.5.cloned.1.call-update) | async-done | bytes 2621456 | tf_op jit(solution)/shard_map/all_gather | solution.py:220
  160.8 10.8 %shard_map.131 = f32[8,512]{1,0:T(8,128)} custom-call(s32[1]{0:T(128)} %copy.15.length_ref, bf16[512,2560]{1,0:T(8,128)(2,1)} %bitcast.21, bf16[16,2560]{1,0:T(8,128)(2,1)} %copy-done.3, f32[1,2560]{1,0:T(1,128)} %broadcast_in_dim.32.gain_ref, bf16[2560,512]{1,0:T(8,128)(2,1)} %all-gather.5.cloned.1.call-done.w_ref, f32[4,2560]{1,0:T(4,128)} %conv_ref.3, ...), custom_call_target="tpu_custom_call" | custom-call | flops 1610612736 | bytes 5242880 | tf_op jit(solution)/shard_map/pallas_call | solution.py:161
  171.6 0.7 pad_maximum_fusion.1
  172.3 5.2 %all_gather.11 = f32[16,2560]{1,0:T(8,128)S(1)} all-gather(f32[8,2560]{1,0:T(8,128)S(1)} %pad_maximum_fusion.1), channel_id=1, replica_groups=mesh['batch'=16,'seq'=2] {'seq'}, dimensions={0}, use_global_device_ids=true | all-gather | bytes 245760 | tf_op jit(solution)/shard_map/all_gather | solution.py:231
  177.5 0.7 fusion.18
  178.2 0.7 dynamic-slice_add_fusion.1
  (18 shorter events, 0.2 us)
Async XLA Ops:
  7.2 4.5 %copy-start = (bf16[2560,512]{1,0:T(8,128)(2,1)S(1)}, bf16[2560,512]{1,0:T(8,128)(2,1)}, u32[]{:S(2)}) copy-start(bf16[2560,512]{1,0:T(8,128)(2,1)} %param.21) | copy-start | bytes 7864324
  7.2 4.5 %copy-start.7 = (f32[2560]{0:T(1024)S(1)}, f32[2560]{0:T(1024)}, u32[]{:S(2)}) copy-start(f32[2560]{0:T(1024)} %param.15) | copy-start | bytes 30724
  7.2 94.3 %all-gather.3.cloned.1.call-start = ((), (), s32[]{:S(2)}) async-start(), calls=%async_computation.1 | async-start | bytes 10813440 | tf_op jit(solution)/shard_map/all_gather | solution.py:218
  9.1 2.5 %copy-start.1 = (bf16[1,512,2560]{2,1,0:T(8,128)(2,1)S(1)}, bf16[1,512,2560]{2,1,0:T(8,128)(2,1)}, u32[]{:S(2)}) copy-start(bf16[1,512,2560]{2,1,0:T(8,128)(2,1)} %param.12) | copy-start | bytes 7864324
  13.3 1.0 copy-start.2
  16.6 86.4 %copy-start.5 = (f32[2560]{0:T(1024)S(1)}, f32[2560]{0:T(1024)}, u32[]{:S(2)}) copy-start(f32[2560]{0:T(1024)} %param.20) | copy-start | bytes 30724
  16.6 87.1 %copy-start.6 = (f32[2560]{0:T(1024)S(1)}, f32[2560]{0:T(1024)}, u32[]{:S(2)}) copy-start(f32[2560]{0:T(1024)} %param.14) | copy-start | bytes 30724
  17.5 15.3 %all-to-all-start = ((bf16[512,2,256]{0,2,1:T(8,128)(2,1)}), bf16[512,2,256]{0,2,1:T(8,128)(2,1)S(1)}, u32[]{:S(2)}, u32[]{:S(2)}) async-start(bf16[512,2,256]{0,2,1:T(8,128)(2,1)} %broadcast_select_fusion), calls=%async_computation | async-start | bytes 1048576 | tf_op jit(solution)/shard_map/all_to_all | solution.py:212
  21.7 139.0 %all-gather.5.cloned.1.call-start = ((), (), s32[]{:S(2)}) async-start(), calls=%async_computation.2 | async-start | bytes 2703360 | tf_op jit(solution)/shard_map/all_gather | solution.py:220
  22.7 13.3 %collective-permute-start = (bf16[16,2560]{1,0:T(8,128)(2,1)S(1)}, bf16[16,2560]{1,0:T(8,128)(2,1)S(1)}, u32[]{:S(2)}, u32[]{:S(2)}) collective-permute-start(bf16[16,2560]{1,0:T(8,128)(2,1)S(1)} %slice_bitcast_fusion), channel_id=1, source_target_pairs={{0,1},{2,3},{4,5},{6,7},{8,9},{10,11},{12,13},{14,15},{16,17},{18,... | collective-permute-start | bytes 245768 | tf_op jit(solution)/shard_map/ppermute | solution.py:22
  35.9 68.4 %copy-start.3 = (bf16[16,2560]{1,0:T(8,128)(2,1)}, bf16[16,2560]{1,0:T(8,128)(2,1)S(1)}, u32[]{:S(2)}) copy-start(bf16[16,2560]{1,0:T(8,128)(2,1)S(1)} %collective-permute-done.halo_ref) | copy-start | bytes 245764
  129.6 41.9 %copy-start.4 = (f32[8,2048]{1,0:T(8,128)S(1)}, f32[8,2048]{1,0:T(8,128)}, u32[]{:S(2)}) copy-start(f32[8,2048]{1,0:T(8,128)} %shard_map.130) | copy-start | bytes 196612
Sparse Core Ops, SparseCore 0:
  10.9 90.5 all-gather.2
  104.4 56.3 all-gather.4
